TPU v7x, 128 devices: a whole 4x4x4 slice. The times are simulated.
128 devices in a mesh: wide: 8 (over z, x_hi), narrow: 4 (over y), depth: 4 (over x_lo, core).
Axes of the slice: x: 4 (x_hi: 2, x_lo: 2; x = x_hi * 2 + x_lo), y: 4, z: 4, core: 2. Of those that a mesh axis runs over, the one named last changes fastest.
Arguments:
- hidden_in: bfloat16 [2048, 4096], P(('wide', 'narrow'), 'depth'), may hold values from -36 to 36
- queries: bfloat16 [2048, 4096], P('wide', ('narrow', 'depth')), may hold values from -8 to 8
- lang_ids: int32 [2048], replicated, may hold values from 0 to 7
- owner_slot: int32 [8], replicated, may hold values from 0 to 7, each once
- enc_kv: bfloat16 [8, 2, 768, 4096], P('wide', None, None, ('narrow', 'depth')), may hold values from -7 to 7
- attn_proj: bfloat16 [4096, 4096], P(('narrow', 'depth')), may hold values from -0.09375 to 0.09375
- norm_gain: float32 [4096], replicated, may hold values from 0.25 to 1.75
- router_proj: float32 [4096, 4], replicated, may hold values from -0.09375 to 0.09375
- expert_ids: int32 [2048, 2], P('wide'), may hold values from 0 to 3, all different within a row; in each aligned block of 64 rows (0 to 63, 64 to 127, ...) at most 48 rows name the same one
- proj_in: bfloat16 [4, 4096, 5120], P('narrow', None, 'depth'), may hold values from -0.09375 to 0.09375
- proj_out: bfloat16 [4, 5120, 4096], P('narrow', 'depth'), may hold values from -0.078125 to 0.078125
Outputs:
- layer_out: bfloat16 [2048, 4096], P(('wide', 'narrow'), 'depth')
Inputs may be any that keep to these rules, and one draw needn't show every extreme that they name: `owner_slot`: every slot once. `expert_ids`: each row names two different experts. Within each aligned block of 64 rows (the rows of one index of wide+narrow) no expert is named more than 48 times, a bound that some block reaches.
All inputs are finite; a program needn't handle non-finite values.
Results may differ from a plain program's by a relative error of at most 0.017.
Values may be sent and summed in bfloat16 or wider, within the bound.
No kernel may reach another device: no remote copies, remote signals or barrier semaphores. Data moves between devices by JAX's collectives and lax.ppermute only.
A program may use at most 128 MiB of HBM per device.

v0:
```python
import math
import jax
import jax.numpy as jnp
from jax import lax
from jax.sharding import PartitionSpec as P

HEAD_DIM = 64
CAP = 48
neg_big = -1e30
norm_eps = 1e-06


def in_order(blocks, dim):
    shape = list(blocks.shape[1:])
    shape[dim] *= blocks.shape[0]
    return jnp.moveaxis(blocks, 0, dim).reshape(shape)


def sent_to_all(value, axis):
    peers = lax.axis_size(axis)
    return lax.all_to_all(
        jnp.broadcast_to(value[None], (peers, *value.shape)), axis, 0, 0, tiled=True
    )


def collect(value, axis, dim):
    return in_order(sent_to_all(value, axis), dim)


def in_blocks(value, dim, peers):
    before, after = (value.shape[:dim], value.shape[dim + 1 :])
    return jnp.moveaxis(value.reshape(*before, peers, -1, *after), dim, 0)


def sum_at_owner(value, axis, dim):
    blocks = in_blocks(value, dim, lax.axis_size(axis))
    arrived = lax.all_to_all(blocks, axis, split_axis=0, concat_axis=0, tiled=True)
    return arrived.astype(jnp.float32).sum(axis=0)


def empty_state(row_count, head_count):
    return (
        jnp.full((row_count, head_count), neg_big, jnp.float32),
        jnp.zeros((row_count, head_count), jnp.float32),
        jnp.zeros((row_count, head_count, HEAD_DIM), jnp.float32),
    )


def slot_update(running, query_rows, key_rows, value_rows, is_live):
    run_max, run_sum, run_acc = running
    scores = jnp.einsum(
        "rhd,khd->rhk", query_rows, key_rows, preferred_element_type=jnp.float32
    ) * HEAD_DIM ** (-0.5)
    new_max = jnp.where(is_live[:, None], jnp.maximum(run_max, jnp.max(scores, axis=2)), run_max)
    weights = jnp.where(is_live[:, None, None], jnp.exp(scores - new_max[:, :, None]), 0.0)
    shrink = jnp.exp(run_max - new_max)
    run_sum = run_sum * shrink + jnp.sum(weights, axis=2)
    taken_sum = jnp.einsum(
        "rhk,khd->rhd", weights.astype(jnp.bfloat16), value_rows, preferred_element_type=jnp.float32
    )
    return (new_max, run_sum, run_acc * shrink[:, :, None] + taken_sum)


def slot_scan(running, kv_block, first_slot, query_rows, slot_tags):
    head_count = query_rows.shape[1]

    def visit_slot(carried, element):
        kv_pair, position = element
        key_rows = kv_pair[0].reshape(kv_pair.shape[1], head_count, HEAD_DIM)
        value_rows = kv_pair[1].reshape(kv_pair.shape[1], head_count, HEAD_DIM)
        return (slot_update(carried, query_rows, key_rows, value_rows, slot_tags == position), None)

    positions = first_slot + jnp.arange(kv_block.shape[0], dtype=jnp.int32)
    running, _ = lax.scan(visit_slot, running, (kv_block, positions))
    return running


def finish(running):
    run_max, run_sum, run_acc = running
    safe_sum = jnp.where(run_sum > 0.0, run_sum, 1.0)
    return (run_acc / safe_sum[:, :, None]).reshape(run_acc.shape[0], -1)


def assign_slots(choice_ids, experts):
    pick_flags = (
        choice_ids[:, :, None] == jnp.arange(experts, dtype=jnp.int32)[None, None, :]
    ).astype(jnp.int32)
    flat_flags = pick_flags.reshape(-1, experts)
    before = jnp.cumsum(flat_flags, axis=0) - flat_flags
    slot_rank = jnp.sum(before * flat_flags, axis=1).reshape(choice_ids.shape)
    return choice_ids * CAP + slot_rank


def make_worker(proj_in, proj_out, depth_count, quarter):
    experts_here = proj_in.shape[0]
    out_blocks = proj_out.reshape(experts_here, proj_out.shape[1], depth_count, quarter)

    def expert_ffn(arrived):
        sources = arrived.shape[0] // experts_here
        slot_count = arrived.shape[1]
        grid_rows = arrived.reshape(sources, experts_here, slot_count, arrived.shape[2])
        hidden_act = jnp.einsum(
            "secd,edf->secf", grid_rows, proj_in, preferred_element_type=jnp.float32
        )
        hidden_act = jax.nn.gelu(hidden_act, approximate=True).astype(jnp.bfloat16)
        expert_part = jnp.einsum(
            "secf,efgq->gsecq", hidden_act, out_blocks, preferred_element_type=jnp.float32
        )
        expert_part = expert_part.reshape(depth_count, sources * experts_here, slot_count, quarter)
        return expert_part

    return expert_ffn


def shards(
    hidden_in,
    queries,
    lang_ids,
    owner_slot,
    enc_kv,
    attn_proj,
    norm_gain,
    router_proj,
    expert_ids,
    proj_in,
    proj_out,
):
    narrow_count = lax.axis_size("narrow")
    depth_count = lax.axis_size("depth")
    tok_rows = hidden_in.shape[0]
    quarter = hidden_in.shape[1]
    head_count = queries.shape[1] // HEAD_DIM
    lang_count = owner_slot.shape[0]
    experts_here = proj_in.shape[0]
    experts = experts_here * narrow_count
    lang_match = lang_ids[:, None] == jnp.arange(lang_count, dtype=jnp.int32)[None, :]
    holder = jnp.sum(jnp.where(lang_match, owner_slot[None, :], 0), axis=1)
    first_slot = lax.axis_index("wide") * enc_kv.shape[0]
    segment = collect(queries, "wide", 0)
    row_count = segment.shape[0]
    block_rows = math.gcd(row_count, 512)

    def one_block(element):
        part_rows, part_tags = element
        running = slot_scan(
            empty_state(block_rows, head_count),
            enc_kv,
            first_slot,
            part_rows.reshape(block_rows, head_count, HEAD_DIM),
            part_tags,
        )
        return finish(running)

    blocks_out = lax.map(
        one_block,
        (
            segment.reshape(row_count // block_rows, block_rows, segment.shape[1]),
            holder.reshape(row_count // block_rows, block_rows),
        ),
    )
    partial_context = blocks_out.reshape(row_count, segment.shape[1])
    context = sum_at_owner(partial_context.astype(jnp.bfloat16), "wide", 0).astype(jnp.bfloat16)
    context_blocks = context.reshape(narrow_count, tok_rows, context.shape[1])
    proj_blocks = attn_proj.reshape(attn_proj.shape[0], depth_count, quarter)

    def pair_term(pair_index):
        row_block = lax.dynamic_index_in_dim(
            context_blocks, pair_index // depth_count, 0, keepdims=False
        )
        col_block = lax.dynamic_index_in_dim(
            proj_blocks, pair_index % depth_count, 1, keepdims=False
        )
        return jnp.dot(row_block, col_block, preferred_element_type=jnp.float32)

    pair_ids = jnp.arange(
        tok_rows * lax.axis_size(("narrow", "depth")) // tok_rows, dtype=jnp.int32
    )
    attn_out = sum_at_owner(
        lax.map(pair_term, pair_ids)
        .reshape(tok_rows * lax.axis_size(("narrow", "depth")), quarter)
        .astype(jnp.bfloat16),
        ("narrow", "depth"),
        0,
    )
    residual = (hidden_in.astype(jnp.float32) + attn_out).astype(jnp.bfloat16)
    full_rows = lax.all_gather(residual, "depth", axis=1, tiled=True).astype(jnp.float32)
    inv_norm = lax.rsqrt(jnp.mean(full_rows * full_rows, axis=1) + norm_eps)
    normed = (full_rows * inv_norm[:, None] * norm_gain[None, :]).astype(jnp.bfloat16)
    narrow_at = lax.axis_index("narrow")
    own_ids = lax.dynamic_slice_in_dim(expert_ids, narrow_at * tok_rows, tok_rows, 0)
    targets = assign_slots(own_ids, experts)
    lane_ids = jnp.arange(experts * CAP, dtype=jnp.int32)
    dispatch_mask = jnp.any(lane_ids[:, None, None] == targets[None, :, :], axis=2).astype(
        jnp.bfloat16
    )
    outbox = jnp.dot(dispatch_mask, normed, preferred_element_type=jnp.float32).astype(jnp.bfloat16)
    outbox = outbox.reshape(experts, CAP, normed.shape[1])
    worker = make_worker(proj_in, proj_out, depth_count, quarter)
    arrived_out = worker(lax.all_to_all(outbox, "narrow", split_axis=0, concat_axis=0, tiled=True))
    summed = sum_at_owner(arrived_out.astype(jnp.bfloat16), "depth", 0)
    returned = lax.all_to_all(
        summed.astype(jnp.bfloat16), "narrow", split_axis=1, concat_axis=1, tiled=True
    ).astype(summed.dtype)
    logits = jnp.dot(normed.astype(jnp.float32), router_proj, precision=lax.Precision.HIGHEST)
    pick_mask = own_ids[:, :, None] == jnp.arange(experts, dtype=jnp.int32)[None, None, :]
    own_logit = jnp.sum(jnp.where(pick_mask, logits[:, None, :], 0.0), axis=2)
    gates = jax.nn.sigmoid(own_logit - own_logit[:, ::-1])
    picked = jnp.take(
        returned.reshape(experts * CAP, quarter), targets.reshape(-1), axis=0
    ).reshape(tok_rows, 2, quarter)
    combined = jnp.sum(gates[:, :, None] * picked, axis=1)
    return (residual.astype(jnp.float32) + combined).astype(jnp.bfloat16)


def solution(mesh):
    return jax.shard_map(
        shards,
        mesh=mesh,
        in_specs=(
            P(("wide", "narrow"), "depth"),
            P("wide", ("narrow", "depth")),
            P(),
            P(),
            P("wide", None, None, ("narrow", "depth")),
            P(("narrow", "depth"), None),
            P(),
            P(),
            P("wide", None),
            P("narrow", None, "depth"),
            P("narrow", "depth", None),
        ),
        out_specs=P(("wide", "narrow"), "depth"),
        check_vma=False,
    )
```

profile of v0, /device:TPU:0, one launch (start us, length us, event | category | flops | bytes accessed | tf_op | source)
XLA Modules:
  0.0 258.0 jit_solution(7034597366299841906)
XLA Ops:
  0.0 2.0 broadcast_in_dim.114
  2.0 7.9 %all-to-all-start = ((bf16[8,256,256]{2,1,0:T(8,128)(2,1)}), bf16[8,256,256]{2,1,0:T(8,128)(2,1)S(1)}, u32[]{:S(2)}, u32[]{:S(2)}) async-start(bf16[8,256,256]{2,1,0:T(8,128)(2,1)} %broadcast_in_dim.114), calls=%async_computation | async-start | bytes 2097152 | tf_op jit(solution)/shard_map/all_to_all | solution.py:21
  12.1 15.0 %all-to-all-done = bf16[8,256,256]{2,1,0:T(8,128)(2,1)S(1)} async-done(((bf16[8,256,256]{2,1,0:T(8,128)(2,1)}), bf16[8,256,256]{2,1,0:T(8,128)(2,1)S(1)}, u32[]{:S(2)}, u32[]{:S(2)}) %all-to-all-start) | async-done | bytes 1048608 | tf_op jit(solution)/shard_map/all_to_all | solution.py:21
  27.1 20.3 %while.28 = (s32[]{:T(128)}, bf16[4,512,256]{2,1,0:T(8,128)(2,1)S(1)}, s32[4,512]{1,0:T(4,128)S(1)}, s32[]{:T(128)}, bf16[4,512,256]{2,1,0:T(8,128)(2,1)S(1)}, /*index=5*/bf16[1,2,768,256]{2,3,1,0:T(8,128)(2,1)S(1)}, s32[]{:T(128)}) while((s32[]{:T(128)}, bf16[4,512,256]{2,1,0:T(8,128)(2,1)S(1)}, s32[4,512]{1,0:T(4,128)S(1)}, s32[]{:T(128)}, ...), condition=%wide.region_4.5_spmd, body=%wide.region_1.4_spmd.sunk | while | flops 418789888 | bytes 23957604 | solution.py:154
  30.2 1.8 fusion.95
  35.3 1.8 fusion.95
  40.3 1.8 fusion.95
  48.4 3.6 %all-to-all-start.1 = ((bf16[8,256,256]{2,1,0:T(8,128)(2,1)}), bf16[8,256,256]{2,1,0:T(8,128)(2,1)S(1)}, u32[]{:S(2)}, u32[]{:S(2)}) async-start(bf16[8,256,256]{2,1,0:T(8,128)(2,1)} %bitcast.143), calls=%async_computation.1 | async-start | bytes 2097152 | tf_op jit(solution)/shard_map/all_to_all | solution.py:37
  51.9 3.3 %copy.53 = bf16[256,4096]{0,1:T(8,128)(2,1)S(1)} copy(bf16[256,4096]{1,0:T(8,128)(2,1)} %param.20) | data formatting | bytes 4194304 | tf_op args[5]
  55.2 13.2 %all-to-all-done.1 = bf16[8,256,256]{2,1,0:T(8,128)(2,1)S(1)} async-done(((bf16[8,256,256]{2,1,0:T(8,128)(2,1)}), bf16[8,256,256]{2,1,0:T(8,128)(2,1)S(1)}, u32[]{:S(2)}, u32[]{:S(2)}) %all-to-all-start.1) | async-done | bytes 1048608 | tf_op jit(solution)/shard_map/all_to_all | solution.py:37
  68.6 64.6 %while.29 = (s32[]{:T(128)}, bf16[16,64,1024]{2,1,0:T(8,128)(2,1)}, s32[16]{0:T(128)S(1)}, bf16[4,64,256]{2,1,0:T(8,128)(2,1)S(1)}, bf16[256,4,1024]{0,2,1:T(8,1...) while((s32[]{:T(128)}, bf16[16,64,1024]{2,1,0:T(8,128)(2,1)}, ...), condition=%wide.region_7.8_spmd, body=%wide.region_6.7_spmd.sunk | while | flops 33554456 | bytes 819596 | solution.py:179
  133.3 4.6 %all-to-all-start.2 = ((bf16[16,64,1024]{2,1,0:T(8,128)(2,1)}), bf16[16,64,1024]{2,1,0:T(8,128)(2,1)S(1)}, u32[]{:S(2)}, u32[]{:S(2)}) async-start(bf16[16,64,1024]{2,1,0:T(8,128)(2,1)} %get-tuple-element.130), calls=%async_computation.2 | async-start | bytes 4194304 | tf_op jit(solution)/shard_map/all_to_all | solution.py:37
  139.1 26.6 %all-to-all-done.2 = bf16[16,64,1024]{2,1,0:T(8,128)(2,1)S(1)} async-done(((bf16[16,64,1024]{2,1,0:T(8,128)(2,1)}), bf16[16,64,1024]{2,1,0:T(8,128)(2,1)S(1)}, u32[]{:S(2)}, u32[]{:S(2)}) %all-to-all-start.2) | async-done | bytes 2097184 | tf_op jit(solution)/shard_map/all_to_all | solution.py:37
  166.1 6.5 %all_gather.3 = bf16[64,4096]{1,0:T(8,128)(2,1)S(1)} all-gather(bf16[64,1024]{1,0:T(8,128)(2,1)S(1)} %add_convert_fusion.1), channel_id=1, replica_groups=mesh['wide'=8,'narrow'=4,'depth'=4] {'depth'}, dimensions={1}, use_global_device_ids=true | all-gather | bytes 655360 | tf_op jit(solution)/shard_map/all_gather | solution.py:186
  172.8 1.8 convolution_convert_fusion
  174.6 3.7 %all-to-all-start.3 = ((bf16[4,48,4096]{2,1,0:T(8,128)(2,1)}), bf16[4,48,4096]{2,1,0:T(8,128)(2,1)S(1)}, u32[]{:S(2)}, u32[]{:S(2)}) async-start(bf16[4,48,4096]{2,1,0:T(8,128)(2,1)} %bitcast.14), calls=%async_computation.3 | async-start | bytes 3145728 | tf_op jit(solution)/shard_map/all_to_all | solution.py:199
  178.4 17.8 %reshape.205 = bf16[1280,4,1024]{2,1,0:T(4,128)(2,1)} reshape(bf16[1,1280,4096]{2,1,0:T(8,128)(2,1)} %param.25) | data formatting | bytes 20971520 | tf_op jit(solution)/shard_map/reshape.14
  196.2 3.5 %all-to-all-done.3 = bf16[4,48,4096]{2,1,0:T(8,128)(2,1)S(1)} async-done(((bf16[4,48,4096]{2,1,0:T(8,128)(2,1)}), bf16[4,48,4096]{2,1,0:T(8,128)(2,1)S(1)}, u32[]{:S(2)}, u32[]{:S(2)}) %all-to-all-start.3) | async-done | bytes 1572896 | tf_op jit(solution)/shard_map/all_to_all | solution.py:199
  199.7 16.7 %fusion.35 = bf16[4,1,4,48,1024]{4,3,0,2,1:T(8,128)(2,1)} fusion(bf16[1280,4,1024]{2,1,0:T(4,128)(2,1)} %reshape.205, bf16[4,48,4096]{2,1,0:T(8,128)(2,1)S(1)} %all-to-all-done.3, bf16[1,4096,1280]{2,1,0:T(8,128)(2,1)} %param.24), kind=kOutput, calls=%fused_computation.36 | convolution fusion | flops 4029530112 | bytes 24117248 | tf_op jit(solution)/shard_map/secf,efgq->gsecq/dot_general | solution.py:106
  216.4 2.7 %copy.60 = bf16[4,1,4,48,1024]{4,3,2,1,0:T(8,128)(2,1)} copy(bf16[4,1,4,48,1024]{4,3,0,2,1:T(8,128)(2,1)} %fusion.35) | data formatting | bytes 3145728 | tf_op jit(solution)/shard_map/convert_element_type | solution.py:200
  219.1 3.6 %all-to-all-start.4 = ((bf16[4,1,4,48,1024]{4,3,2,1,0:T(8,128)(2,1)}), bf16[4,1,4,48,1024]{4,3,2,1,0:T(8,128)(2,1)S(1)}, u32[]{:S(2)}, u32[]{:S(2)}) async-start(bf16[4,1,4,48,1024]{4,3,2,1,0:T(8,128)(2,1)} %copy.60), calls=%async_computation.4 | async-start | bytes 3145728 | tf_op jit(solution)/shard_map/all_to_all | solution.py:37
  223.6 19.0 %all-to-all-done.4 = bf16[4,1,4,48,1024]{4,3,2,1,0:T(8,128)(2,1)S(1)} async-done(((bf16[4,1,4,48,1024]{4,3,2,1,0:T(8,128)(2,1)}), bf16[4,1,4,48,1024]{4,3,2,1,0:T(8,128)(2,1)S(1)}, u32[]{:S(2)}, u32[]{:S(2)}) %all-to-all-start.4) | async-done | bytes 1572896 | tf_op jit(solution)/shard_map/all_to_all | solution.py:37
  243.8 3.5 %all-to-all-start.5 = ((bf16[1,4,48,1024]{3,2,0,1:T(8,128)(2,1)}), bf16[1,4,48,1024]{3,2,0,1:T(8,128)(2,1)S(1)}, u32[]{:S(2)}, u32[]{:S(2)}) async-start(bf16[1,4,48,1024]{3,2,0,1:T(8,128)(2,1)} %bitcast.30), calls=%async_computation.5 | async-start | bytes 786432 | tf_op jit(solution)/shard_map/all_to_all | solution.py:201
  247.4 7.9 %all-to-all-done.5 = bf16[1,4,48,1024]{3,2,0,1:T(8,128)(2,1)S(1)} async-done(((bf16[1,4,48,1024]{3,2,0,1:T(8,128)(2,1)}), bf16[1,4,48,1024]{3,2,0,1:T(8,128)(2,1)S(1)}, u32[]{:S(2)}, u32[]{:S(2)}) %all-to-all-start.5) | async-done | bytes 393248 | tf_op jit(solution)/shard_map/all_to_all | solution.py:201
  (120 shorter events, 49.3 us)
Async XLA Ops:
  0.0 223.0 %copy-start = (f32[4096,4]{0,1:T(4,128)S(1)}, f32[4096,4]{0,1:T(4,128)}, u32[]{:S(2)}) copy-start(f32[4096,4]{0,1:T(4,128)} %param.22) | copy-start | bytes 196612
  2.0 25.1 %all-to-all-start = ((bf16[8,256,256]{2,1,0:T(8,128)(2,1)}), bf16[8,256,256]{2,1,0:T(8,128)(2,1)S(1)}, u32[]{:S(2)}, u32[]{:S(2)}) async-start(bf16[8,256,256]{2,1,0:T(8,128)(2,1)} %broadcast_in_dim.114), calls=%async_computation | async-start | bytes 2097152 | tf_op jit(solution)/shard_map/all_to_all | solution.py:21
  47.4 1.0 copy-start.1
  48.4 20.1 %all-to-all-start.1 = ((bf16[8,256,256]{2,1,0:T(8,128)(2,1)}), bf16[8,256,256]{2,1,0:T(8,128)(2,1)S(1)}, u32[]{:S(2)}, u32[]{:S(2)}) async-start(bf16[8,256,256]{2,1,0:T(8,128)(2,1)} %bitcast.143), calls=%async_computation.1 | async-start | bytes 2097152 | tf_op jit(solution)/shard_map/all_to_all | solution.py:37
  51.9 85.9 %copy-start.4 = (s32[256,2]{0,1:T(2,128)S(1)}, s32[256,2]{0,1:T(2,128)}, u32[]{:S(2)}) copy-start(s32[256,2]{0,1:T(2,128)} %param.23) | copy-start | bytes 6148
  55.2 110.8 %copy-start.2 = (bf16[64,1024]{1,0:T(8,128)(2,1)S(1)}, bf16[64,1024]{1,0:T(8,128)(2,1)}, u32[]{:S(2)}) copy-start(bf16[64,1024]{1,0:T(8,128)(2,1)} %param.15) | copy-start | bytes 393220
  68.6 104.2 %copy-start.3 = (f32[4096]{0:T(1024)S(1)}, f32[4096]{0:T(1024)}, u32[]{:S(2)}) copy-start(f32[4096]{0:T(1024)} %param.21) | copy-start | bytes 49156
  133.3 32.4 %all-to-all-start.2 = ((bf16[16,64,1024]{2,1,0:T(8,128)(2,1)}), bf16[16,64,1024]{2,1,0:T(8,128)(2,1)S(1)}, u32[]{:S(2)}, u32[]{:S(2)}) async-start(bf16[16,64,1024]{2,1,0:T(8,128)(2,1)} %get-tuple-element.130), calls=%async_computation.2 | async-start | bytes 4194304 | tf_op jit(solution)/shard_map/all_to_all | solution.py:37
  174.6 25.0 %all-to-all-start.3 = ((bf16[4,48,4096]{2,1,0:T(8,128)(2,1)}), bf16[4,48,4096]{2,1,0:T(8,128)(2,1)S(1)}, u32[]{:S(2)}, u32[]{:S(2)}) async-start(bf16[4,48,4096]{2,1,0:T(8,128)(2,1)} %bitcast.14), calls=%async_computation.3 | async-start | bytes 3145728 | tf_op jit(solution)/shard_map/all_to_all | solution.py:199
  219.1 23.6 %all-to-all-start.4 = ((bf16[4,1,4,48,1024]{4,3,2,1,0:T(8,128)(2,1)}), bf16[4,1,4,48,1024]{4,3,2,1,0:T(8,128)(2,1)S(1)}, u32[]{:S(2)}, u32[]{:S(2)}) async-start(bf16[4,1,4,48,1024]{4,3,2,1,0:T(8,128)(2,1)} %copy.60), calls=%async_computation.4 | async-start | bytes 3145728 | tf_op jit(solution)/shard_map/all_to_all | solution.py:37
  243.8 11.5 %all-to-all-start.5 = ((bf16[1,4,48,1024]{3,2,0,1:T(8,128)(2,1)}), bf16[1,4,48,1024]{3,2,0,1:T(8,128)(2,1)S(1)}, u32[]{:S(2)}, u32[]{:S(2)}) async-start(bf16[1,4,48,1024]{3,2,0,1:T(8,128)(2,1)} %bitcast.30), calls=%async_computation.5 | async-start | bytes 786432 | tf_op jit(solution)/shard_map/all_to_all | solution.py:201
where the time goes:
time: 260 us; the launch traced here: 258 us
  waiting for transfers between devices  85.2 us (33%)
  matrix products  45.8 us (18%)
  local copies, waits for them, and re-layouts  41.3 us (16%)
  loops' own time  40.3 us (15%)
  starting transfers between devices  26.8 us (10%)
  other arithmetic  11.9 us (5%)
  blocking collectives  6.5 us (2%)
    all_to_all x3, waiting for transfers between devices, sum_at_owner(): lax.all_to_all(blocks, axis, split_axis=0, concat_axis=0, tiled=True)  58.9 us
    another operation x1, loops' own time, shards(): lax.map(pair_term, pair_ids)  40.1 us
    another operation x1, local copies, waits for them, and re-layouts  17.8 us
    dot_general x1, matrix products, expert_ffn(): jnp.einsum('secf,efgq->gsecq', hidden_act, out_blocks, preferred_element_...  16.7 us
    dot_general x16, matrix products, pair_term(): return jnp.dot(row_block, col_block, preferred_element_type=jnp.float32)  15.1 us
    all_to_all x1, waiting for transfers between devices, sent_to_all(): lax.all_to_all(jnp.broadcast_to(value[None], (peers, *value.shape)), axis...  15 us
    all_to_all x3, starting transfers between devices, sum_at_owner(): lax.all_to_all(blocks, axis, split_axis=0, concat_axis=0, tiled=True)  11.7 us
    dynamic_slice x16, local copies, waits for them, and re-layouts, shards(): lax.map(pair_term, pair_ids)  9.44 us
  transfers between devices with their start and end apart: 6, of which 6 were waited for; matrix products, arithmetic and copies ran while one was open for 10% of the time, Pallas kernels for 0%

commit v1 on v0

--- a/solution.py
+++ b/solution.py
@@ -183,7 +183,9 @@
         0,
     )
     residual = (hidden_in.astype(jnp.float32) + attn_out).astype(jnp.bfloat16)
-    full_rows = lax.all_gather(residual, "depth", axis=1, tiled=True).astype(jnp.float32)
+    full_rows = jnp.concatenate(
+        lax.all_to_all(jnp.stack([residual] * lax.axis_size("depth")), "depth", 0, 0), axis=1
+    ).astype(jnp.float32)
     inv_norm = lax.rsqrt(jnp.mean(full_rows * full_rows, axis=1) + norm_eps)
     normed = (full_rows * inv_norm[:, None] * norm_gain[None, :]).astype(jnp.bfloat16)
     narrow_at = lax.axis_index("narrow")

time: 260 us -> 271 us (1.042)
  waiting for transfers between devices: 85.2 us -> 93.4 us
  blocking collectives: 6.5 us -> 0 us
  starting transfers between devices: 26.8 us -> 32 us
  local copies, waits for them, and re-layouts: 41.3 us -> 44.1 us
    all_to_all x0 -> x1, waiting for transfers between devices: none -> 8.19 us  [shards(): lax.all_to_all(jnp.stack([residual] * lax.axis_size('depth')), 'depth', 0...]
    all_gather x1 -> x0, blocking collectives: 6.5 us -> none  [shards(): lax.all_gather(residual, 'depth', axis=1, tiled=True).astype(jnp.float32)]
    all_to_all x0 -> x1, starting transfers between devices: none -> 3.47 us  [shards(): lax.all_to_all(jnp.stack([residual] * lax.axis_size('depth')), 'depth', 0...]
    dynamic_update_slice x8, local copies, waits for them, and re-layouts: 0.63 us -> 3.47 us  [shards(): lax.map(one_block, (segment.reshape(row_count // block_rows, block_rows,...]
    another operation x1 -> x2, local copies, waits for them, and re-layouts: 17.8 us -> 18.7 us
  transfers between devices with their start and end apart: 6 -> 7, of which waited for: 6 -> 7; matrix products, arithmetic and copies ran while one was open for 10% -> 9% of each run, Pallas kernels for 0% -> 0%
where the time goes in v1:
time: 271 us; the launch traced here: 270 us
  waiting for transfers between devices  93.4 us (34%)
  matrix products  46.3 us (17%)
  local copies, waits for them, and re-layouts  44.1 us (16%)
  loops' own time  40.3 us (15%)
  starting transfers between devices  32 us (12%)
  other arithmetic  13.4 us (5%)
    all_to_all x3, waiting for transfers between devices, sum_at_owner(): lax.all_to_all(blocks, axis, split_axis=0, concat_axis=0, tiled=True)  59.6 us
    another operation x1, loops' own time, shards(): lax.map(pair_term, pair_ids)  40 us
    another operation x1, local copies, waits for them, and re-layouts  17.8 us
    dot_general x1, matrix products, expert_ffn(): jnp.einsum('secf,efgq->gsecq', hidden_act, out_blocks, preferred_element_...  17.2 us
    dot_general x16, matrix products, pair_term(): return jnp.dot(row_block, col_block, preferred_element_type=jnp.float32)  15.1 us
    all_to_all x1, waiting for transfers between devices, sent_to_all(): lax.all_to_all(jnp.broadcast_to(value[None], (peers, *value.shape)), axis...  15 us
    all_to_all x3, starting transfers between devices, sum_at_owner(): lax.all_to_all(blocks, axis, split_axis=0, concat_axis=0, tiled=True)  12.6 us
    dynamic_slice x16, local copies, waits for them, and re-layouts, shards(): lax.map(pair_term, pair_ids)  9.44 us
  transfers between devices with their start and end apart: 7, of which 7 were waited for; matrix products, arithmetic and copies ran while one was open for 9% of the time, Pallas kernels for 0%

profile of v1, /device:TPU:0, one launch (start us, length us, event | category | flops | bytes accessed | tf_op | source)
XLA Modules:
  0.0 269.7 jit_solution(4706272069725545494)
XLA Ops:
  0.0 2.0 broadcast_in_dim.114
  2.0 7.9 %all-to-all-start = ((bf16[8,256,256]{2,1,0:T(8,128)(2,1)}), bf16[8,256,256]{2,1,0:T(8,128)(2,1)S(1)}, u32[]{:S(2)}, u32[]{:S(2)}) async-start(bf16[8,256,256]{2,1,0:T(8,128)(2,1)} %broadcast_in_dim.114), calls=%async_computation | async-start | bytes 2097152 | tf_op jit(solution)/shard_map/all_to_all | solution.py:21
  12.1 15.0 %all-to-all-done = bf16[8,256,256]{2,1,0:T(8,128)(2,1)S(1)} async-done(((bf16[8,256,256]{2,1,0:T(8,128)(2,1)}), bf16[8,256,256]{2,1,0:T(8,128)(2,1)S(1)}, u32[]{:S(2)}, u32[]{:S(2)}) %all-to-all-start) | async-done | bytes 1048608 | tf_op jit(solution)/shard_map/all_to_all | solution.py:21
  27.1 23.0 %while.28 = (s32[]{:T(128)}, bf16[4,512,256]{2,1,0:T(8,128)(2,1)}, s32[4,512]{1,0:T(4,128)S(1)}, s32[]{:T(128)}, bf16[4,512,256]{2,1,0:T(8,128)(2,1)S(1)}, /*index=5*/bf16[1,2,768,256]{2,3,1,0:T(8,128)(2,1)S(1)}, s32[]{:T(128)}) while((s32[]{:T(128)}, bf16[4,512,256]{2,1,0:T(8,128)(2,1)}, s32[4,512]{1,0:T(4,128)S(1)}, s32[]{:T(128)}, ...), condition=%wide.region_4.5_spmd, body=%wide.region_1.4_spmd.sunk | while | flops 418789888 | bytes 23957604 | solution.py:154
  35.9 1.8 fusion.91
  50.1 3.6 %all-to-all-start.1 = ((bf16[8,256,256]{2,1,0:T(8,128)(2,1)}), bf16[8,256,256]{2,1,0:T(8,128)(2,1)S(1)}, u32[]{:S(2)}, u32[]{:S(2)}) async-start(bf16[8,256,256]{2,1,0:T(8,128)(2,1)} %bitcast.150), calls=%async_computation.1 | async-start | bytes 2097152 | tf_op jit(solution)/shard_map/all_to_all | solution.py:37
  53.7 3.3 %copy.55 = bf16[256,4096]{0,1:T(8,128)(2,1)S(1)} copy(bf16[256,4096]{1,0:T(8,128)(2,1)} %param.20) | data formatting | bytes 4194304 | tf_op args[5]
  56.9 13.2 %all-to-all-done.1 = bf16[8,256,256]{2,1,0:T(8,128)(2,1)S(1)} async-done(((bf16[8,256,256]{2,1,0:T(8,128)(2,1)}), bf16[8,256,256]{2,1,0:T(8,128)(2,1)S(1)}, u32[]{:S(2)}, u32[]{:S(2)}) %all-to-all-start.1) | async-done | bytes 1048608 | tf_op jit(solution)/shard_map/all_to_all | solution.py:37
  70.3 64.6 %while.29 = (s32[]{:T(128)}, bf16[16,64,1024]{2,1,0:T(8,128)(2,1)}, s32[16]{0:T(128)S(1)}, bf16[4,64,256]{2,1,0:T(8,128)(2,1)S(1)}, bf16[256,4,1024]{0,2,1:T(8,1...) while((s32[]{:T(128)}, bf16[16,64,1024]{2,1,0:T(8,128)(2,1)}, ...), condition=%wide.region_7.8_spmd, body=%wide.region_6.7_spmd.sunk | while | flops 33554456 | bytes 819596 | solution.py:179
  135.0 4.7 %all-to-all-start.2 = ((bf16[16,64,1024]{2,1,0:T(8,128)(2,1)}), bf16[16,64,1024]{2,1,0:T(8,128)(2,1)S(1)}, u32[]{:S(2)}, u32[]{:S(2)}) async-start(bf16[16,64,1024]{2,1,0:T(8,128)(2,1)} %get-tuple-element.130), calls=%async_computation.2 | async-start | bytes 4194304 | tf_op jit(solution)/shard_map/all_to_all | solution.py:37
  140.3 27.2 %all-to-all-done.2 = bf16[16,64,1024]{2,1,0:T(8,128)(2,1)S(1)} async-done(((bf16[16,64,1024]{2,1,0:T(8,128)(2,1)}), bf16[16,64,1024]{2,1,0:T(8,128)(2,1)S(1)}, u32[]{:S(2)}, u32[]{:S(2)}) %all-to-all-start.2) | async-done | bytes 2097184 | tf_op jit(solution)/shard_map/all_to_all | solution.py:37
  168.8 3.5 %all-to-all-start.3 = ((bf16[4,64,1024]{2,1,0:T(8,128)(2,1)}), bf16[4,64,1024]{2,1,0:T(8,128)(2,1)S(1)}, u32[]{:S(2)}, u32[]{:S(2)}) async-start(bf16[4,64,1024]{2,1,0:T(8,128)(2,1)} %stack.2), calls=%async_computation.3 | async-start | bytes 1048576 | tf_op jit(solution)/shard_map/all_to_all | solution.py:187
  172.9 8.2 %all-to-all-done.3 = bf16[4,64,1024]{2,1,0:T(8,128)(2,1)S(1)} async-done(((bf16[4,64,1024]{2,1,0:T(8,128)(2,1)}), bf16[4,64,1024]{2,1,0:T(8,128)(2,1)S(1)}, u32[]{:S(2)}, u32[]{:S(2)}) %all-to-all-start.3) | async-done | bytes 524320 | tf_op jit(solution)/shard_map/all_to_all | solution.py:187
  181.5 1.9 convolution_convert_fusion
  183.4 4.5 %all-to-all-start.4 = ((bf16[4,48,4096]{2,1,0:T(8,128)(2,1)}), bf16[4,48,4096]{2,1,0:T(8,128)(2,1)}, u32[]{:S(2)}, u32[]{:S(2)}) async-start(bf16[4,48,4096]{2,1,0:T(8,128)(2,1)} %bitcast.148), calls=%async_computation.4 | async-start | bytes 3145728 | tf_op jit(solution)/shard_map/all_to_all | solution.py:201
  187.9 17.8 %reshape.211 = bf16[1280,4,1024]{2,1,0:T(4,128)(2,1)} reshape(bf16[1,1280,4096]{2,1,0:T(8,128)(2,1)} %param.25) | data formatting | bytes 20971520 | tf_op jit(solution)/shard_map/reshape.15
  205.8 2.8 %all-to-all-done.4 = bf16[4,48,4096]{2,1,0:T(8,128)(2,1)} async-done(((bf16[4,48,4096]{2,1,0:T(8,128)(2,1)}), bf16[4,48,4096]{2,1,0:T(8,128)(2,1)}, u32[]{:S(2)}, u32[]{:S(2)}) %all-to-all-start.4) | async-done | bytes 1572896 | tf_op jit(solution)/shard_map/all_to_all | solution.py:201
  208.5 17.2 %fusion.35 = bf16[4,1,4,48,1024]{4,3,0,2,1:T(8,128)(2,1)} fusion(bf16[1280,4,1024]{2,1,0:T(4,128)(2,1)} %reshape.211, bf16[4,48,4096]{2,1,0:T(8,128)(2,1)} %all-to-all-done.4, bf16[1,4096,1280]{2,1,0:T(8,128)(2,1)} %param.24), kind=kOutput, calls=%fused_computation.36 | convolution fusion | flops 4029530112 | bytes 24117248 | tf_op jit(solution)/shard_map/secf,efgq->gsecq/dot_general | solution.py:106
  225.8 2.7 %copy.63 = bf16[4,1,4,48,1024]{4,3,2,1,0:T(8,128)(2,1)} copy(bf16[4,1,4,48,1024]{4,3,0,2,1:T(8,128)(2,1)} %fusion.35) | data formatting | bytes 3145728 | tf_op jit(solution)/shard_map/convert_element_type | solution.py:202
  228.5 4.3 %all-to-all-start.5 = ((bf16[4,1,4,48,1024]{4,3,2,1,0:T(8,128)(2,1)}), bf16[4,1,4,48,1024]{4,3,2,1,0:T(8,128)(2,1)}, u32[]{:S(2)}, u32[]{:S(2)}) async-start(bf16[4,1,4,48,1024]{4,3,2,1,0:T(8,128)(2,1)} %copy.63), calls=%async_computation.5 | async-start | bytes 3145728 | tf_op jit(solution)/shard_map/all_to_all | solution.py:37
  233.8 19.2 %all-to-all-done.5 = bf16[4,1,4,48,1024]{4,3,2,1,0:T(8,128)(2,1)} async-done(((bf16[4,1,4,48,1024]{4,3,2,1,0:T(8,128)(2,1)}), bf16[4,1,4,48,1024]{4,3,2,1,0:T(8,128)(2,1)}, u32[]{:S(2)}, u32[]{:S(2)}) %all-to-all-start.5) | async-done | bytes 1572896 | tf_op jit(solution)/shard_map/all_to_all | solution.py:37
  252.9 2.6 reduce_sum.96
  255.5 3.5 %all-to-all-start.6 = ((bf16[1,4,48,1024]{3,2,0,1:T(8,128)(2,1)}), bf16[1,4,48,1024]{3,2,0,1:T(8,128)(2,1)S(1)}, u32[]{:S(2)}, u32[]{:S(2)}) async-start(bf16[1,4,48,1024]{3,2,0,1:T(8,128)(2,1)} %bitcast.31), calls=%async_computation.6 | async-start | bytes 786432 | tf_op jit(solution)/shard_map/all_to_all | solution.py:203
  259.1 7.9 %all-to-all-done.6 = bf16[1,4,48,1024]{3,2,0,1:T(8,128)(2,1)S(1)} async-done(((bf16[1,4,48,1024]{3,2,0,1:T(8,128)(2,1)}), bf16[1,4,48,1024]{3,2,0,1:T(8,128)(2,1)S(1)}, u32[]{:S(2)}, u32[]{:S(2)}) %all-to-all-start.6) | async-done | bytes 393248 | tf_op jit(solution)/shard_map/all_to_all | solution.py:203
  (122 shorter events, 54.6 us)
Async XLA Ops:
  0.0 233.2 %copy-start = (f32[4096,4]{0,1:T(4,128)S(1)}, f32[4096,4]{0,1:T(4,128)}, u32[]{:S(2)}) copy-start(f32[4096,4]{0,1:T(4,128)} %param.22) | copy-start | bytes 196612
  2.0 25.1 %all-to-all-start = ((bf16[8,256,256]{2,1,0:T(8,128)(2,1)}), bf16[8,256,256]{2,1,0:T(8,128)(2,1)S(1)}, u32[]{:S(2)}, u32[]{:S(2)}) async-start(bf16[8,256,256]{2,1,0:T(8,128)(2,1)} %broadcast_in_dim.114), calls=%async_computation | async-start | bytes 2097152 | tf_op jit(solution)/shard_map/all_to_all | solution.py:21
  50.1 20.1 %all-to-all-start.1 = ((bf16[8,256,256]{2,1,0:T(8,128)(2,1)}), bf16[8,256,256]{2,1,0:T(8,128)(2,1)S(1)}, u32[]{:S(2)}, u32[]{:S(2)}) async-start(bf16[8,256,256]{2,1,0:T(8,128)(2,1)} %bitcast.150), calls=%async_computation.1 | async-start | bytes 2097152 | tf_op jit(solution)/shard_map/all_to_all | solution.py:37
  53.6 86.1 %copy-start.3 = (s32[256,2]{0,1:T(2,128)S(1)}, s32[256,2]{0,1:T(2,128)}, u32[]{:S(2)}) copy-start(s32[256,2]{0,1:T(2,128)} %param.23) | copy-start | bytes 6148
  56.9 111.0 %copy-start.1 = (bf16[64,1024]{1,0:T(8,128)(2,1)S(1)}, bf16[64,1024]{1,0:T(8,128)(2,1)}, u32[]{:S(2)}) copy-start(bf16[64,1024]{1,0:T(8,128)(2,1)} %param.15) | copy-start | bytes 393220
  135.0 46.6 %copy-start.2 = (f32[4096]{0:T(1024)S(1)}, f32[4096]{0:T(1024)}, u32[]{:S(2)}) copy-start(f32[4096]{0:T(1024)} %param.21) | copy-start | bytes 49156
  135.0 32.6 %all-to-all-start.2 = ((bf16[16,64,1024]{2,1,0:T(8,128)(2,1)}), bf16[16,64,1024]{2,1,0:T(8,128)(2,1)S(1)}, u32[]{:S(2)}, u32[]{:S(2)}) async-start(bf16[16,64,1024]{2,1,0:T(8,128)(2,1)} %get-tuple-element.130), calls=%async_computation.2 | async-start | bytes 4194304 | tf_op jit(solution)/shard_map/all_to_all | solution.py:37
  168.8 12.3 %all-to-all-start.3 = ((bf16[4,64,1024]{2,1,0:T(8,128)(2,1)}), bf16[4,64,1024]{2,1,0:T(8,128)(2,1)S(1)}, u32[]{:S(2)}, u32[]{:S(2)}) async-start(bf16[4,64,1024]{2,1,0:T(8,128)(2,1)} %stack.2), calls=%async_computation.3 | async-start | bytes 1048576 | tf_op jit(solution)/shard_map/all_to_all | solution.py:187
  183.4 25.1 %all-to-all-start.4 = ((bf16[4,48,4096]{2,1,0:T(8,128)(2,1)}), bf16[4,48,4096]{2,1,0:T(8,128)(2,1)}, u32[]{:S(2)}, u32[]{:S(2)}) async-start(bf16[4,48,4096]{2,1,0:T(8,128)(2,1)} %bitcast.148), calls=%async_computation.4 | async-start | bytes 3145728 | tf_op jit(solution)/shard_map/all_to_all | solution.py:201
  228.5 24.5 %all-to-all-start.5 = ((bf16[4,1,4,48,1024]{4,3,2,1,0:T(8,128)(2,1)}), bf16[4,1,4,48,1024]{4,3,2,1,0:T(8,128)(2,1)}, u32[]{:S(2)}, u32[]{:S(2)}) async-start(bf16[4,1,4,48,1024]{4,3,2,1,0:T(8,128)(2,1)} %copy.63), calls=%async_computation.5 | async-start | bytes 3145728 | tf_op jit(solution)/shard_map/all_to_all | solution.py:37
  255.5 11.5 %all-to-all-start.6 = ((bf16[1,4,48,1024]{3,2,0,1:T(8,128)(2,1)}), bf16[1,4,48,1024]{3,2,0,1:T(8,128)(2,1)S(1)}, u32[]{:S(2)}, u32[]{:S(2)}) async-start(bf16[1,4,48,1024]{3,2,0,1:T(8,128)(2,1)} %bitcast.31), calls=%async_computation.6 | async-start | bytes 786432 | tf_op jit(solution)/shard_map/all_to_all | solution.py:203
